TPU v7x, 32 devices: a whole 2x2x4 slice. The times are simulated.
32 devices in a mesh: dap: 32 (over z, y, x, core), ch: 1.
Axes of the slice: x: 2, y: 2, z: 4, core: 2. Of those that a mesh axis runs over, the one named last changes fastest.
Arguments:
- alignment_embedding: bfloat16 [128, 128, 256], P(None, 'dap'), may hold values from -6 to 6
- couple_embedding: bfloat16 [128, 128, 128], P('dap', 'ch'), may hold values from -6 to 6
- tensor_first_matrix: bfloat16 [256, 32], P(None, 'ch'), may hold values from -0.375 to 0.375
- tensor_second_matrix: bfloat16 [256, 32], replicated, may hold values from -0.375 to 0.375
- tensor_final_matrix: bfloat16 [1024, 128], P('ch'), may hold values from -1 to 1
- trimul_entry_matrix: bfloat16 [4, 128, 128], replicated, may hold values from -0.5 to 0.5
- trimul_sigmoid_matrix: bfloat16 [128, 128], replicated, may hold values from -0.5 to 0.5
- trimul_final_matrix: bfloat16 [128, 128], replicated, may hold values from -0.5 to 0.5
Outputs:
- pair_out: bfloat16 [128, 128, 128], P('dap', 'ch')
All inputs are finite; a program needn't handle non-finite values.
Results may differ from a plain program's by a relative error of at most 0.014.
Values may be sent and summed in bfloat16 or wider, within the bound.
A program may use at most 64 MiB of HBM per device.

v0:
```python
import jax
import jax.numpy as jnp
from jax import lax
from jax.sharding import PartitionSpec as P


def standardize_fn(value, axis):
    mean = jnp.mean(value, axis=axis, keepdims=True)
    centred = value - mean
    var = jnp.mean(centred * centred, axis=axis, keepdims=True)
    return centred * lax.rsqrt(var + 1e-05)


def outer_update(first_operand, right_rows, w_out, alignment_height):
    rows = first_operand.shape[1]
    outer = jnp.einsum(
        "sic,sje->ijce", first_operand, right_rows, preferred_element_type=jnp.float32
    )
    outer = (outer * (1.0 / alignment_height)).astype(jnp.bfloat16)
    outer = outer.reshape(rows, right_rows.shape[1], first_operand.shape[2] * right_rows.shape[2])
    return jnp.einsum("ijf,fz->ijz", outer, w_out, preferred_element_type=jnp.float32)


def per_device(
    alignment_embedding,
    couple_embedding,
    tensor_first_matrix,
    tensor_second_matrix,
    tensor_final_matrix,
    trimul_entry_matrix,
    trimul_sigmoid_matrix,
    trimul_final_matrix,
):
    alignment_height = alignment_embedding.shape[0]
    columns = couple_embedding.shape[1]
    alignment_standardized = standardize_fn(alignment_embedding.astype(jnp.float32), -1).astype(
        jnp.bfloat16
    )
    second_operand = jnp.einsum(
        "ziv,vl->zil",
        alignment_standardized,
        tensor_second_matrix,
        preferred_element_type=jnp.float32,
    ).astype(jnp.bfloat16)
    right_all = lax.all_gather(second_operand, "dap", axis=1, tiled=True)
    first_operand = jnp.einsum(
        "ziv,vl->zil",
        alignment_standardized,
        tensor_first_matrix,
        preferred_element_type=jnp.float32,
    ).astype(jnp.bfloat16)
    terms = outer_update(first_operand, right_all, tensor_final_matrix, alignment_height)
    totals = lax.psum(terms.astype(jnp.bfloat16), "ch").astype(jnp.float32)
    update = lax.dynamic_slice_in_dim(totals, lax.axis_index("ch") * columns, columns, 1)
    lifted = (couple_embedding.astype(jnp.float32) + update).astype(jnp.bfloat16)
    normed = standardize_fn(lifted.astype(jnp.float32), -1).astype(jnp.bfloat16)
    projected = jnp.einsum(
        "rkz,qzc->qcrk", normed, trimul_entry_matrix, preferred_element_type=jnp.float32
    )
    left_t = (jax.nn.sigmoid(projected[0]) * projected[1]).astype(jnp.bfloat16)
    right_t = (jax.nn.sigmoid(projected[2]) * projected[3]).astype(jnp.bfloat16)
    left_cols, right_cols = (
        lax.all_to_all(left_t, "dap", split_axis=0, concat_axis=1, tiled=True),
        lax.all_to_all(right_t, "dap", split_axis=0, concat_axis=1, tiled=True),
    )
    product = jnp.einsum("cik,cjk->cij", left_cols, right_cols, preferred_element_type=jnp.float32)
    returned = lax.all_to_all(
        product.astype(jnp.bfloat16), "dap", split_axis=1, concat_axis=0, tiled=True
    ).astype(product.dtype)
    summed = lax.psum_scatter(returned.astype(jnp.bfloat16), "ch", scatter_dimension=2, tiled=True)
    tri_n = standardize_fn(summed.astype(jnp.float32), 0).astype(jnp.bfloat16)
    out = jnp.einsum("crj,cz->rjz", tri_n, trimul_final_matrix, preferred_element_type=jnp.float32)
    gate = jax.nn.sigmoid(
        jnp.einsum("rjz,zy->rjy", normed, trimul_sigmoid_matrix, preferred_element_type=jnp.float32)
    )
    return (lifted.astype(jnp.float32) + gate * out).astype(jnp.bfloat16)


def solution(mesh):
    placed = (
        P(None, "dap", None),
        P("dap", "ch", None),
        P(None, "ch"),
        P(),
        P("ch", None),
        P(),
        P(),
        P(),
    )
    return jax.shard_map(
        per_device, mesh=mesh, in_specs=placed, out_specs=P("dap", "ch", None), check_vma=False
    )
```

profile of v0, /device:TPU:0, one launch (start us, length us, event | category | flops | bytes accessed | tf_op | source)
XLA Modules:
  0.0 114.2 jit_solution(17043596067753059552)
XLA Ops:
  6.5 0.0 copy-start
  6.5 0.0 copy-start.1
  6.5 0.0 copy-start.7
  6.5 0.0 copy-start.2
  6.5 0.0 all-gather.2.cloned.1.call-start
  6.6 1.2 %convert_reduce_fusion = f32[128,4]{1,0:T(8,128)S(1)} fusion(bf16[128,4,256]{2,1,0:T(4,128)(2,1)} %param.8), kind=kLoop, calls=%fused_computation.21 | loop fusion | flops 261632 | bytes 264192 | tf_op jit(solution)/shard_map/reduce_sum | solution.py:8
  7.8 0.0 copy-start.5
  7.8 1.3 %fusion.14 = f32[128,4]{1,0:T(8,128)S(1)} fusion(bf16[128,4,256]{2,1,0:T(4,128)(2,1)} %param.8, f32[128,4]{1,0:T(8,128)S(1)} %broadcast_multiply_fusion), kind=kLoop, calls=%fused_computation.24 | loop fusion | flops 523776 | bytes 266240 | tf_op jit(solution)/shard_map/reduce_sum | solution.py:10
  9.2 0.0 copy-done.1
  9.2 0.3 fusion.15
  9.6 0.0 copy-done.7
  9.6 0.8 convolution_convert_fusion.3
  10.4 0.0 all-gather.2.cloned.1.call-update
  10.4 0.0 copy-done.2
  10.4 0.1 copy.34
  10.5 56.3 %all-gather.2.cloned.1.call-done = bf16[128,128,32]{0,2,1:T(8,128)(2,1)} async-done(((bf16[128,4,32]{0,2,1:T(8,128)(2,1)}), bf16[128,128,32]{0,2,1:T(8,128)(2,1)}) %all-gather.2.cloned.1.call-update) | async-done | bytes 1048592 | tf_op jit(solution)/shard_map/all_gather | solution.py:45
  66.9 0.0 copy-done.5
  66.9 1.9 %fusion = bf16[4,128,32,32]{1,2,0,3:T(8,128)(2,1)S(1)} fusion(bf16[128,128,32,1]{0,2,1,3:T(8,128)(2,1)} %bitcast.65, bf16[128,4,256]{2,1,0:T(4,128)(2,1)S(1)} %fusion.15, bf16[256,32]{0,1:T(8,128)(2,1)S(1)} %copy-done.5), kind=kOutput, calls=%fused_computation.1 | convolution fusion | flops 143671296 | bytes 2375680 | tf_op jit(solution)/shard_map/sic,sje->ijce/dot_general | solution.py:16
  68.8 0.7 copy.38
  69.5 0.0 copy-start.3
  69.5 0.0 copy-done
  69.5 0.4 fusion.41
  69.9 0.5 copy-done.3
  70.4 0.3 convolution_bitcast_fusion
  70.7 0.1 fusion.35
  70.9 0.8 copy.47
  71.6 3.6 %all-to-all-start.1 = ((bf16[128,4,128]{2,1,0:T(4,128)(2,1)}), bf16[128,4,128]{2,1,0:T(4,128)(2,1)S(1)}, u32[]{:S(2)}, u32[]{:S(2)}) async-start(bf16[128,4,128]{2,1,0:T(4,128)(2,1)} %copy.47), calls=%async_computation.1 | async-start | bytes 262144 | tf_op jit(solution)/shard_map/all_to_all | solution.py:64
  75.2 0.8 copy.44
  76.0 7.4 %all-to-all-done.1 = bf16[128,4,128]{2,1,0:T(4,128)(2,1)S(1)} async-done(((bf16[128,4,128]{2,1,0:T(4,128)(2,1)}), bf16[128,4,128]{2,1,0:T(4,128)(2,1)S(1)}, u32[]{:S(2)}, u32[]{:S(2)}) %all-to-all-start.1) | async-done | bytes 131104 | tf_op jit(solution)/shard_map/all_to_all | solution.py:64
  83.4 2.6 %all-to-all-start = ((bf16[128,4,128]{2,1,0:T(4,128)(2,1)}), bf16[128,4,128]{2,1,0:T(4,128)(2,1)S(1)}, u32[]{:S(2)}, u32[]{:S(2)}) async-start(bf16[128,4,128]{2,1,0:T(4,128)(2,1)} %copy.44), calls=%async_computation | async-start | bytes 262144 | tf_op jit(solution)/shard_map/all_to_all | solution.py:63
  86.0 0.0 copy-start.6
  86.1 0.1 copy.49
  86.2 8.1 %all-to-all-done = bf16[128,4,128]{2,1,0:T(4,128)(2,1)S(1)} async-done(((bf16[128,4,128]{2,1,0:T(4,128)(2,1)}), bf16[128,4,128]{2,1,0:T(4,128)(2,1)S(1)}, u32[]{:S(2)}, u32[]{:S(2)}) %all-to-all-start) | async-done | bytes 131104 | tf_op jit(solution)/shard_map/all_to_all | solution.py:63
  94.2 0.1 copy.46
  94.3 0.2 convolution_convert_fusion
  94.6 0.8 copy.50
  95.3 2.6 %all-to-all-start.2 = ((bf16[4,128,128]{2,0,1:T(4,128)(2,1)}), bf16[4,128,128]{2,0,1:T(4,128)(2,1)S(1)}, u32[]{:S(2)}, u32[]{:S(2)}) async-start(bf16[4,128,128]{2,0,1:T(4,128)(2,1)} %copy.50), calls=%async_computation.2 | async-start | bytes 262144 | tf_op jit(solution)/shard_map/all_to_all | solution.py:67
  97.9 0.0 copy-done.6
  97.9 0.0 copy-start.4
  97.9 0.3 fusion.4
  98.2 7.9 %all-to-all-done.2 = bf16[4,128,128]{2,0,1:T(4,128)(2,1)S(1)} async-done(((bf16[4,128,128]{2,0,1:T(4,128)(2,1)}), bf16[4,128,128]{2,0,1:T(4,128)(2,1)S(1)}, u32[]{:S(2)}, u32[]{:S(2)}) %all-to-all-start.2) | async-done | bytes 131104 | tf_op jit(solution)/shard_map/all_to_all | solution.py:67
  106.1 0.1 bitcast_reduce_fusion
  106.2 0.1 fusion.25
  106.3 0.0 copy-done.4
  106.4 0.2 fusion.5
  106.6 0.8 copy.54
  (11 shorter events, 0.2 us)
Async XLA Ops:
  6.5 63.0 %copy-start = (bf16[1024,128]{1,0:T(8,128)(2,1)S(1)}, bf16[1024,128]{1,0:T(8,128)(2,1)}, u32[]{:S(2)}) copy-start(bf16[1024,128]{1,0:T(8,128)(2,1)} %param.12) | copy-start | bytes 786436
  6.5 2.7 %copy-start.1 = (bf16[128,4,256]{2,1,0:T(4,128)(2,1)S(1)}, bf16[128,4,256]{2,1,0:T(4,128)(2,1)}, u32[]{:S(2)}) copy-start(bf16[128,4,256]{2,1,0:T(4,128)(2,1)} %param.8) | copy-start | bytes 786436
  6.5 3.0 %copy-start.7 = (bf16[256,32]{0,1:T(8,128)(2,1)S(1)}, bf16[256,32]{0,1:T(8,128)(2,1)}, u32[]{:S(2)}) copy-start(bf16[256,32]{0,1:T(8,128)(2,1)} %param.11) | copy-start | bytes 49156
  6.5 3.9 %copy-start.2 = (bf16[4,128,128]{2,1,0:T(8,128)(2,1)S(1)}, bf16[4,128,128]{2,1,0:T(8,128)(2,1)}, u32[]{:S(2)}) copy-start(bf16[4,128,128]{2,1,0:T(8,128)(2,1)} %param.9) | copy-start | bytes 393220
  6.5 60.3 %all-gather.2.cloned.1.call-start = ((), (), s32[]{:S(2)}) async-start(), calls=%async_computation.3 | async-start | bytes 1081344 | tf_op jit(solution)/shard_map/all_gather | solution.py:45
  7.8 59.1 %copy-start.5 = (bf16[256,32]{0,1:T(8,128)(2,1)S(1)}, bf16[256,32]{0,1:T(8,128)(2,1)}, u32[]{:S(2)}) copy-start(bf16[256,32]{0,1:T(8,128)(2,1)} %param.10) | copy-start | bytes 49156
  69.5 0.9 copy-start.3
  71.6 11.8 %all-to-all-start.1 = ((bf16[128,4,128]{2,1,0:T(4,128)(2,1)}), bf16[128,4,128]{2,1,0:T(4,128)(2,1)S(1)}, u32[]{:S(2)}, u32[]{:S(2)}) async-start(bf16[128,4,128]{2,1,0:T(4,128)(2,1)} %copy.47), calls=%async_computation.1 | async-start | bytes 262144 | tf_op jit(solution)/shard_map/all_to_all | solution.py:64
  83.4 10.8 %all-to-all-start = ((bf16[128,4,128]{2,1,0:T(4,128)(2,1)}), bf16[128,4,128]{2,1,0:T(4,128)(2,1)S(1)}, u32[]{:S(2)}, u32[]{:S(2)}) async-start(bf16[128,4,128]{2,1,0:T(4,128)(2,1)} %copy.44), calls=%async_computation | async-start | bytes 262144 | tf_op jit(solution)/shard_map/all_to_all | solution.py:63
  86.0 11.9 %copy-start.6 = (bf16[128,128]{1,0:T(8,128)(2,1)S(1)}, bf16[128,128]{1,0:T(8,128)(2,1)}, u32[]{:S(2)}) copy-start(bf16[128,128]{1,0:T(8,128)(2,1)} %param.14) | copy-start | bytes 98308
  95.3 10.8 %all-to-all-start.2 = ((bf16[4,128,128]{2,0,1:T(4,128)(2,1)}), bf16[4,128,128]{2,0,1:T(4,128)(2,1)S(1)}, u32[]{:S(2)}, u32[]{:S(2)}) async-start(bf16[4,128,128]{2,0,1:T(4,128)(2,1)} %copy.50), calls=%async_computation.2 | async-start | bytes 262144 | tf_op jit(solution)/shard_map/all_to_all | solution.py:67
  97.9 8.4 %copy-start.4 = (bf16[128,128]{1,0:T(8,128)(2,1)S(1)}, bf16[128,128]{1,0:T(8,128)(2,1)}, u32[]{:S(2)}) copy-start(bf16[128,128]{1,0:T(8,128)(2,1)} %param.15) | copy-start | bytes 98308
Sparse Core Ops, SparseCore 0:
  10.5 56.3 all-gather.1
where the time goes:
time: 115 us; the launch traced here: 114 us
  waiting for transfers between devices  79.7 us (69%)
  between operations  13.7 us (12%)
  starting transfers between devices  8.77 us (8%)
  local copies, waits for them, and re-layouts  4.68 us (4%)
  matrix products  4.1 us (4%)
  other arithmetic  3.28 us (3%)
    all_gather x1, waiting for transfers between devices, per_device(): right_all = lax.all_gather(second_operand, 'dap', axis=1, tiled=True)  56.3 us
    all_to_all x1, waiting for transfers between devices, per_device(): lax.all_to_all(left_t, 'dap', split_axis=0, concat_axis=1, tiled=True)  8.05 us
    all_to_all x1, waiting for transfers between devices, per_device(): lax.all_to_all(product.astype(jnp.bfloat16), 'dap', split_axis=1, concat_...  7.91 us
    all_to_all x1, waiting for transfers between devices, per_device(): lax.all_to_all(right_t, 'dap', split_axis=0, concat_axis=1, tiled=True)  7.41 us
    all_to_all x1, starting transfers between devices, per_device(): lax.all_to_all(right_t, 'dap', split_axis=0, concat_axis=1, tiled=True)  3.58 us
    all_to_all x1, starting transfers between devices, per_device(): lax.all_to_all(left_t, 'dap', split_axis=0, concat_axis=1, tiled=True)  2.58 us
    all_to_all x1, starting transfers between devices, per_device(): lax.all_to_all(product.astype(jnp.bfloat16), 'dap', split_axis=1, concat_...  2.58 us
  transfers between devices with their start and end apart: 4, of which 4 were waited for; matrix products, arithmetic and copies ran while one was open for 1% of the time, Pallas kernels for 0%

commit v1 on v0

--- a/solution.py
+++ b/solution.py
@@ -61,7 +61,12 @@
     right_t = (jax.nn.sigmoid(projected[2]) * projected[3]).astype(jnp.bfloat16)
     left_cols, right_cols = (
         lax.all_to_all(left_t, "dap", split_axis=0, concat_axis=1, tiled=True),
-        lax.all_to_all(right_t, "dap", split_axis=0, concat_axis=1, tiled=True),
+        jnp.concatenate(
+            lax.all_to_all(
+                jnp.stack(jnp.split(right_t, lax.axis_size("dap"), axis=0)), "dap", 0, 0
+            ),
+            axis=1,
+        ),
     )
     product = jnp.einsum("cik,cjk->cij", left_cols, right_cols, preferred_element_type=jnp.float32)
     returned = lax.all_to_all(

time: 115 us -> 114 us (level)
  no operation moved by 1% of the time
where the time goes in v1:
time: 114 us
  waiting for transfers between devices  79.3 us (70%)
  between operations  13.8 us (12%)
  starting transfers between devices  8.75 us (8%)
  local copies, waits for them, and re-layouts  4.83 us (4%)
  matrix products  4.11 us (4%)
  other arithmetic  3.28 us (3%)
    all_gather x1, waiting for transfers between devices, per_device(): right_all = lax.all_gather(second_operand, 'dap', axis=1, tiled=True)  56.3 us
    all_to_all x1, waiting for transfers between devices, per_device(): lax.all_to_all(jnp.stack(jnp.split(right_t, lax.axis_size('dap'), axis=0)...  8.15 us
    all_to_all x1, waiting for transfers between devices, per_device(): lax.all_to_all(product.astype(jnp.bfloat16), 'dap', split_axis=1, concat_...  7.91 us
    all_to_all x1, waiting for transfers between devices, per_device(): lax.all_to_all(left_t, 'dap', split_axis=0, concat_axis=1, tiled=True)  6.93 us
    all_to_all x1, starting transfers between devices, per_device(): lax.all_to_all(left_t, 'dap', split_axis=0, concat_axis=1, tiled=True)  3.58 us
    all_to_all x1, starting transfers between devices, per_device(): lax.all_to_all(product.astype(jnp.bfloat16), 'dap', split_axis=1, concat_...  2.58 us
    all_to_all x1, starting transfers between devices, per_device(): lax.all_to_all(jnp.stack(jnp.split(right_t, lax.axis_size('dap'), axis=0)...  2.56 us
  transfers between devices with their start and end apart: 4, of which 4 were waited for; matrix products, arithmetic and copies ran while one was open for 1% of the time, Pallas kernels for 0%

profile of v1, /device:TPU:0, one launch (start us, length us, event | category | flops | bytes accessed | tf_op | source)
XLA Modules:
  0.0 114.1 jit_solution(2523740966811021534)
XLA Ops:
  6.5 0.0 copy-start
  6.5 0.0 copy-start.1
  6.5 0.0 copy-start.7
  6.5 0.0 copy-start.2
  6.5 0.0 all-gather.2.cloned.1.call-start
  6.6 1.2 %convert_reduce_fusion = f32[128,4]{1,0:T(8,128)S(1)} fusion(bf16[128,4,256]{2,1,0:T(4,128)(2,1)} %param.8), kind=kLoop, calls=%fused_computation.21 | loop fusion | flops 261632 | bytes 264192 | tf_op jit(solution)/shard_map/reduce_sum | solution.py:8
  7.8 0.0 copy-start.5
  7.8 1.3 %fusion.14 = f32[128,4]{1,0:T(8,128)S(1)} fusion(bf16[128,4,256]{2,1,0:T(4,128)(2,1)} %param.8, f32[128,4]{1,0:T(8,128)S(1)} %broadcast_multiply_fusion), kind=kLoop, calls=%fused_computation.24 | loop fusion | flops 523776 | bytes 266240 | tf_op jit(solution)/shard_map/reduce_sum | solution.py:10
  9.2 0.0 copy-done.1
  9.2 0.3 fusion.15
  9.6 0.0 copy-done.7
  9.6 0.8 convolution_convert_fusion.3
  10.4 0.0 all-gather.2.cloned.1.call-update
  10.4 0.0 copy-done.2
  10.4 0.1 copy.33
  10.5 56.3 %all-gather.2.cloned.1.call-done = bf16[128,128,32]{0,2,1:T(8,128)(2,1)} async-done(((bf16[128,4,32]{0,2,1:T(8,128)(2,1)}), bf16[128,128,32]{0,2,1:T(8,128)(2,1)}) %all-gather.2.cloned.1.call-update) | async-done | bytes 1048592 | tf_op jit(solution)/shard_map/all_gather | solution.py:45
  66.9 0.0 copy-done.5
  66.9 1.9 %fusion = bf16[4,128,32,32]{1,2,0,3:T(8,128)(2,1)S(1)} fusion(bf16[128,128,32,1]{0,2,1,3:T(8,128)(2,1)} %bitcast.61, bf16[128,4,256]{2,1,0:T(4,128)(2,1)S(1)} %fusion.15, bf16[256,32]{0,1:T(8,128)(2,1)S(1)} %copy-done.5), kind=kOutput, calls=%fused_computation.1 | convolution fusion | flops 143671296 | bytes 2375680 | tf_op jit(solution)/shard_map/sic,sje->ijce/dot_general | solution.py:16
  68.8 0.7 copy.37
  69.5 0.0 copy-start.3
  69.5 0.0 copy-done
  69.5 0.4 fusion.40
  69.9 0.5 copy-done.3
  70.4 0.3 convolution_bitcast_fusion
  70.7 0.1 fusion.16
  70.9 0.8 copy.44
  71.6 3.6 %all-to-all-start = ((bf16[128,4,128]{2,1,0:T(4,128)(2,1)}), bf16[128,4,128]{2,1,0:T(4,128)(2,1)S(1)}, u32[]{:S(2)}, u32[]{:S(2)}) async-start(bf16[128,4,128]{2,1,0:T(4,128)(2,1)} %copy.44), calls=%async_computation | async-start | bytes 262144 | tf_op jit(solution)/shard_map/all_to_all | solution.py:63
  75.5 0.0 copy-start.6
  75.8 0.7 copy.46
  76.5 6.9 %all-to-all-done = bf16[128,4,128]{2,1,0:T(4,128)(2,1)S(1)} async-done(((bf16[128,4,128]{2,1,0:T(4,128)(2,1)}), bf16[128,4,128]{2,1,0:T(4,128)(2,1)S(1)}, u32[]{:S(2)}, u32[]{:S(2)}) %all-to-all-start) | async-done | bytes 131104 | tf_op jit(solution)/shard_map/all_to_all | solution.py:63
  83.4 2.6 %all-to-all-start.1 = ((bf16[32,4,4,128]{3,1,2,0:T(4,128)(2,1)}), bf16[32,4,4,128]{3,1,2,0:T(4,128)(2,1)S(1)}, u32[]{:S(2)}, u32[]{:S(2)}) async-start(bf16[32,4,4,128]{3,1,2,0:T(4,128)(2,1)} %copy.46), calls=%async_computation.1 | async-start | bytes 262144 | tf_op jit(solution)/shard_map/all_to_all | solution.py:65
  86.1 8.1 %all-to-all-done.1 = bf16[32,4,4,128]{3,1,2,0:T(4,128)(2,1)S(1)} async-done(((bf16[32,4,4,128]{3,1,2,0:T(4,128)(2,1)}), bf16[32,4,4,128]{3,1,2,0:T(4,128)(2,1)S(1)}, u32[]{:S(2)}, u32[]{:S(2)}) %all-to-all-start.1) | async-done | bytes 131104 | tf_op jit(solution)/shard_map/all_to_all | solution.py:65
  94.2 0.1 copy.47
  94.3 0.2 convolution_convert_fusion
  94.5 0.8 copy.48
  95.2 2.6 %all-to-all-start.2 = ((bf16[4,128,128]{2,0,1:T(4,128)(2,1)}), bf16[4,128,128]{2,0,1:T(4,128)(2,1)S(1)}, u32[]{:S(2)}, u32[]{:S(2)}) async-start(bf16[4,128,128]{2,0,1:T(4,128)(2,1)} %copy.48), calls=%async_computation.2 | async-start | bytes 262144 | tf_op jit(solution)/shard_map/all_to_all | solution.py:72
  97.8 0.0 copy-done.6
  97.8 0.0 copy-start.4
  97.8 0.3 fusion.4
  98.1 7.9 %all-to-all-done.2 = bf16[4,128,128]{2,0,1:T(4,128)(2,1)S(1)} async-done(((bf16[4,128,128]{2,0,1:T(4,128)(2,1)}), bf16[4,128,128]{2,0,1:T(4,128)(2,1)S(1)}, u32[]{:S(2)}, u32[]{:S(2)}) %all-to-all-start.2) | async-done | bytes 131104 | tf_op jit(solution)/shard_map/all_to_all | solution.py:72
  106.0 0.1 bitcast_reduce_fusion
  106.1 0.1 fusion.25
  106.3 0.0 copy-done.4
  106.3 0.2 fusion.5
  106.5 0.8 copy.52
  (42 shorter events, 0.6 us)
Async XLA Ops:
  6.5 63.0 %copy-start = (bf16[1024,128]{1,0:T(8,128)(2,1)S(1)}, bf16[1024,128]{1,0:T(8,128)(2,1)}, u32[]{:S(2)}) copy-start(bf16[1024,128]{1,0:T(8,128)(2,1)} %param.12) | copy-start | bytes 786436
  6.5 2.7 %copy-start.1 = (bf16[128,4,256]{2,1,0:T(4,128)(2,1)S(1)}, bf16[128,4,256]{2,1,0:T(4,128)(2,1)}, u32[]{:S(2)}) copy-start(bf16[128,4,256]{2,1,0:T(4,128)(2,1)} %param.8) | copy-start | bytes 786436
  6.5 3.0 %copy-start.7 = (bf16[256,32]{0,1:T(8,128)(2,1)S(1)}, bf16[256,32]{0,1:T(8,128)(2,1)}, u32[]{:S(2)}) copy-start(bf16[256,32]{0,1:T(8,128)(2,1)} %param.11) | copy-start | bytes 49156
  6.5 3.9 %copy-start.2 = (bf16[4,128,128]{2,1,0:T(8,128)(2,1)S(1)}, bf16[4,128,128]{2,1,0:T(8,128)(2,1)}, u32[]{:S(2)}) copy-start(bf16[4,128,128]{2,1,0:T(8,128)(2,1)} %param.9) | copy-start | bytes 393220
  6.5 60.3 %all-gather.2.cloned.1.call-start = ((), (), s32[]{:S(2)}) async-start(), calls=%async_computation.3 | async-start | bytes 1081344 | tf_op jit(solution)/shard_map/all_gather | solution.py:45
  7.8 59.1 %copy-start.5 = (bf16[256,32]{0,1:T(8,128)(2,1)S(1)}, bf16[256,32]{0,1:T(8,128)(2,1)}, u32[]{:S(2)}) copy-start(bf16[256,32]{0,1:T(8,128)(2,1)} %param.10) | copy-start | bytes 49156
  69.5 0.9 copy-start.3
  71.6 11.8 %all-to-all-start = ((bf16[128,4,128]{2,1,0:T(4,128)(2,1)}), bf16[128,4,128]{2,1,0:T(4,128)(2,1)S(1)}, u32[]{:S(2)}, u32[]{:S(2)}) async-start(bf16[128,4,128]{2,1,0:T(4,128)(2,1)} %copy.44), calls=%async_computation | async-start | bytes 262144 | tf_op jit(solution)/shard_map/all_to_all | solution.py:63
  75.5 22.3 %copy-start.6 = (bf16[128,128]{1,0:T(8,128)(2,1)S(1)}, bf16[128,128]{1,0:T(8,128)(2,1)}, u32[]{:S(2)}) copy-start(bf16[128,128]{1,0:T(8,128)(2,1)} %param.14) | copy-start | bytes 98308
  83.4 10.8 %all-to-all-start.1 = ((bf16[32,4,4,128]{3,1,2,0:T(4,128)(2,1)}), bf16[32,4,4,128]{3,1,2,0:T(4,128)(2,1)S(1)}, u32[]{:S(2)}, u32[]{:S(2)}) async-start(bf16[32,4,4,128]{3,1,2,0:T(4,128)(2,1)} %copy.46), calls=%async_computation.1 | async-start | bytes 262144 | tf_op jit(solution)/shard_map/all_to_all | solution.py:65
  95.2 10.8 %all-to-all-start.2 = ((bf16[4,128,128]{2,0,1:T(4,128)(2,1)}), bf16[4,128,128]{2,0,1:T(4,128)(2,1)S(1)}, u32[]{:S(2)}, u32[]{:S(2)}) async-start(bf16[4,128,128]{2,0,1:T(4,128)(2,1)} %copy.48), calls=%async_computation.2 | async-start | bytes 262144 | tf_op jit(solution)/shard_map/all_to_all | solution.py:72
  97.8 8.4 %copy-start.4 = (bf16[128,128]{1,0:T(8,128)(2,1)S(1)}, bf16[128,128]{1,0:T(8,128)(2,1)}, u32[]{:S(2)}) copy-start(bf16[128,128]{1,0:T(8,128)(2,1)} %param.15) | copy-start | bytes 98308
Sparse Core Ops, SparseCore 0:
  10.5 56.3 all-gather.1
